TPU v7x, 32 devices: a whole 2x2x4 slice. The times are simulated.
32 devices in a mesh: dp: 4 (over y, x), seq: 8 (over z, core).
Axes of the slice: x: 2, y: 2, z: 4, core: 2. Of those that a mesh axis runs over, the one named last changes fastest.
Arguments:
- tokens: bfloat16 [4, 4096, 2560], P('dp', 'seq'), may hold values from -6 to 6
- w_x: bfloat16 [2560, 3072], P('seq'), may hold values from -0.125 to 0.125
- w_bc: bfloat16 [2560, 256], P('seq'), may hold values from -0.125 to 0.125
- w_dt: bfloat16 [2560, 48], P('seq'), may hold values from -0.125 to 0.125
- dt_bias: float32 [48], replicated, may hold values from -1 to 0.5
- decay_rate: float32 [48], replicated, may hold values from 9.765625e-05 to 0.12
- gain: float32 [3072], replicated, may hold values from 0.5 to 1.5
- cotangent: bfloat16 [4, 4096, 3072], P('dp', 'seq'), may hold values from -0.005859375 to 0.005859375
- counts: int32 [8], replicated, may hold values from 1 to 2, 12 in all
Outputs:
- ssm_output: bfloat16 [4, 4096, 3072], P('dp', 'seq')
- grad_c: float32 [2560, 128], P('seq')
Inputs may be any that keep to these rules, and one draw needn't show every extreme that they name: counts add up to 12 and one of them equals 2.
All inputs are finite; a program needn't handle non-finite values.
Results may differ from a plain program's by a relative error of at most 0.02.
Values may be sent and summed in bfloat16 or wider, within the bound.
A program may use at most 128 MiB of HBM per device.

v0:
```python
import jax
import jax.numpy as jnp
from jax import lax
from jax.sharding import PartitionSpec as P

L = 256
norm_floor = 1.0


def entering(value, axis, join, neutral):
    count, mine = (lax.axis_size(axis), lax.axis_index(axis))
    pieces = jax.tree.map(lambda part: lax.all_gather(part, axis), value)
    subtotal = jax.tree.map(
        lambda part, zero: jnp.full_like(part, 0) + jnp.asarray(zero, part.dtype), value, neutral
    )

    def hop(position, subtotal):
        longer = join(subtotal, jax.tree.map(lambda part: part[position], pieces))
        return jax.tree.map(lambda new, old: jnp.where(position < mine, new, old), longer, subtotal)

    return lax.fori_loop(0, count - 1, hop, subtotal)


def scale_state(state, decay):
    return (state.reshape(decay.shape[0], -1) * decay[:, None]).reshape(state.shape)


def combine_states(earlier, later):
    return (earlier[0] * later[0], scale_state(earlier[1], later[0]) + later[1])


def decay_weights(cumulative, dt_rows):
    length = cumulative.shape[0]
    causal = jnp.arange(length)[:, None] >= jnp.arange(length)[None, :]
    gap_log = cumulative.T[:, :, None] - cumulative.T[:, None, :]
    gap_log = jnp.where(causal[None, :, :], gap_log, -jnp.inf)
    return jnp.exp(gap_log) * dt_rows.T[:, None, :]


def stretch_state(inner, b_proj, dt_rows, a_neg):
    length = inner.shape[0]
    head_count = a_neg.shape[0]
    cumulative = jnp.cumsum(dt_rows * a_neg[None, :], axis=0)
    to_end = jnp.exp(cumulative[-1][None, :] - cumulative) * dt_rows
    scaled = (
        (inner.reshape(length, head_count, -1) * to_end[:, :, None])
        .reshape(length, -1)
        .astype(jnp.bfloat16)
    )
    state_add = jnp.dot(scaled.T, b_proj, preferred_element_type=jnp.float32)
    return (jnp.exp(cumulative[-1]), state_add)


def stretch_outputs(inner, b_proj, c_proj, dt_rows, a_neg, state_in, gain, cot_rows, slot_used):
    length = inner.shape[0]
    head_count = a_neg.shape[0]
    head_size = inner.shape[1] // head_count
    cumulative = jnp.cumsum(dt_rows * a_neg[None, :], axis=0)
    weights = decay_weights(cumulative, dt_rows)
    gram_mat = jnp.dot(c_proj, b_proj.T, preferred_element_type=jnp.float32)
    mixing = (gram_mat[None, :, :] * weights).astype(jnp.bfloat16)
    inner_heads = inner.reshape(length, head_count, head_size)
    y_intra = jnp.einsum("hts,shp->thp", mixing, inner_heads, preferred_element_type=jnp.float32)
    state_low = state_in.astype(jnp.bfloat16)
    growth = jnp.exp(cumulative)[:, :, None]
    y_inter = (
        jnp.dot(c_proj, state_low.T, preferred_element_type=jnp.float32).reshape(
            length, head_count, head_size
        )
        * growth
    )
    full = y_intra + y_inter
    radius = jnp.sqrt(jnp.mean(full * full, axis=2, keepdims=True) + norm_floor)
    gain_heads = gain.reshape(head_count, head_size)
    output = (full / radius * gain_heads * slot_used).reshape(length, -1).astype(jnp.bfloat16)
    grad_out = cot_rows.reshape(length, head_count, head_size) * gain_heads
    grad_full = (
        grad_out / radius
        - full * jnp.sum(grad_out * full, axis=2, keepdims=True) / (head_size * radius**3)
    ) * slot_used
    grad_low = grad_full.astype(jnp.bfloat16)
    intersect = jnp.einsum(
        "thp,shp->hts", grad_low, inner_heads, preferred_element_type=jnp.float32
    )
    combined = jnp.sum(intersect * weights, axis=0).astype(jnp.bfloat16)
    grad_intra = jnp.dot(combined, b_proj, preferred_element_type=jnp.float32)
    scaled_grad = (grad_full * growth).reshape(length, -1).astype(jnp.bfloat16)
    grad_inter = jnp.dot(scaled_grad, state_low, preferred_element_type=jnp.float32)
    return (output, (grad_intra + grad_inter).astype(jnp.bfloat16))


def body(tokens, w_x, w_bc, w_dt, dt_bias, decay_rate, gain, cotangent, counts):
    seq_tokens = tokens[0]
    cot_rows = cotangent[0]
    row_total = seq_tokens.shape[0]
    slot_count = row_total // L
    state_size = w_bc.shape[1] // 2
    head_count = decay_rate.shape[0]
    group_index = lax.axis_index("seq")
    filled = jnp.sum(jnp.where(jnp.arange(counts.shape[0]) == group_index, counts, 0))
    slot_used = (jnp.arange(slot_count) < filled).astype(jnp.float32)
    pieces = (
        lax.all_gather(w_x, "seq", axis=0, tiled=True),
        lax.all_gather(w_bc, "seq", axis=0, tiled=True),
        lax.all_gather(w_dt, "seq", axis=0, tiled=True),
    )
    columns = seq_tokens
    inner_sum, bc_raw, dt_raw = tuple(
        (jnp.dot(columns, block_rows, preferred_element_type=jnp.float32) for block_rows in pieces)
    )
    inner = inner_sum.astype(jnp.bfloat16)
    b_proj = bc_raw[:, :state_size].astype(jnp.bfloat16)
    c_proj = bc_raw[:, state_size:].astype(jnp.bfloat16)
    a_neg = -decay_rate
    dt_blocks = (
        jax.nn.softplus(dt_raw + dt_bias).reshape(slot_count, L, head_count)
        * slot_used[:, None, None]
    )
    inner_blocks = inner.reshape(slot_count, L, -1)
    b_blocks = b_proj.reshape(slot_count, L, -1)
    c_blocks = c_proj.reshape(slot_count, L, -1)
    cot_blocks = cot_rows.reshape(slot_count, L, -1)
    decays, additions = lax.map(
        lambda stretch_data: stretch_state(
            stretch_data[0], stretch_data[1], stretch_data[2], a_neg
        ),
        (inner_blocks, b_blocks, dt_blocks),
    )

    def advance(running, stretch_data):
        return (combine_states(running, stretch_data), running)

    starting_state = (
        jnp.ones((head_count,), jnp.float32),
        jnp.zeros(additions.shape[1:], jnp.float32),
    )
    (dev_decay, dev_state), (prior_decay, prior_state) = lax.scan(
        advance, starting_state, (decays, additions)
    )
    unused_decay, state_before = entering(
        (dev_decay, dev_state), "seq", combine_states, starting_state
    )
    state_in = (state_before.reshape(head_count, -1)[None, :, :] * prior_decay[:, :, None]).reshape(
        prior_state.shape
    ) + prior_state
    outputs, grad_blocks = lax.map(
        lambda stretch_data: stretch_outputs(
            stretch_data[0],
            stretch_data[1],
            stretch_data[2],
            stretch_data[3],
            a_neg,
            stretch_data[4],
            gain,
            stretch_data[5],
            stretch_data[6],
        ),
        (inner_blocks, b_blocks, c_blocks, dt_blocks, state_in, cot_blocks, slot_used),
    )
    ssm_output = outputs.reshape(row_total, -1)
    grad_c_rows = grad_blocks.reshape(row_total, -1)
    columns = seq_tokens
    partial_rows = lax.psum_scatter(
        jnp.dot(columns.T, grad_c_rows, preferred_element_type=jnp.float32).astype(jnp.bfloat16),
        "seq",
        scatter_dimension=0,
        tiled=True,
    )
    gradient = lax.psum(partial_rows, "dp").astype(jnp.float32)
    return (ssm_output[None], gradient)


def solution(mesh):
    return jax.shard_map(
        body,
        mesh=mesh,
        in_specs=(
            P("dp", "seq", None),
            P("seq", None),
            P("seq", None),
            P("seq", None),
            P(),
            P(),
            P(),
            P("dp", "seq", None),
            P(),
        ),
        out_specs=(P("dp", "seq", None), P("seq", None)),
        check_vma=False,
    )
```

profile of v0, /device:TPU:0, one launch (start us, length us, event | category | flops | bytes accessed | tf_op | source)
XLA Modules:
  0.0 519.9 jit_solution(12384996486794329397)
XLA Ops:
  8.8 16.2 %all-gather.2 = bf16[8,320,48]{1,2,0:T(8,128)(2,1)S(1)} all-gather(bf16[1,320,48]{1,2,0:T(8,128)(2,1)} %bitcast.250), channel_id=1, replica_groups=mesh['dp'=4,'seq'=8] {'seq'}, dimensions={0}, use_global_device_ids=true | all-gather | bytes 276480 | tf_op jit(solution)/shard_map/all_gather | solution.py:105
  27.6 8.7 %all-gather.9.cloned.1.call-done = bf16[2560,256]{1,0:T(8,128)(2,1)} async-done(((bf16[320,256]{1,0:T(8,128)(2,1)}), bf16[2560,256]{1,0:T(8,128)(2,1)}) %all-gather.9.cloned.1.call-update) | async-done | bytes 1310736 | tf_op jit(solution)/shard_map/all_gather | solution.py:104
  38.6 141.5 %all-gather.7.cloned.1.call-done = bf16[2560,3072]{1,0:T(8,128)(2,1)} async-done(((bf16[320,3072]{1,0:T(8,128)(2,1)}), bf16[2560,3072]{1,0:T(8,128)(2,1)}) %all-gather.7.cloned.1.call-update) | async-done | bytes 15728656 | tf_op jit(solution)/shard_map/all_gather | solution.py:103
  180.1 12.8 %convolution_convert_fusion = bf16[512,3072]{1,0:T(8,128)(2,1)} fusion(bf16[2560,3072]{1,0:T(8,128)(2,1)} %all-gather.7.cloned.1.call-done, bf16[1,512,2560]{2,1,0:T(8,128)(2,1)S(1)} %copy-done), kind=kOutput, calls=%fused_computation.87 | convolution fusion | flops 8054636544 | bytes 21495808 | tf_op jit(solution)/shard_map/dot_general | solution.py:109
  192.9 4.7 copy.52
  199.4 11.9 %while.55 = (s32[]{:T(128)}, f32[2,48]{1,0:T(2,128)S(1)}, f32[2,3072,128]{2,1,0:T(8,128)}, f32[2,256,48]{1,2,0:T(8,128)S(1)}, f32[48]{0:T(128)S(1)}, /*index=5*/...) while((s32[]{:T(128)}, f32[2,48]{1,0:T(2,128)S(1)}, ...), condition=%wide.region_4.5_spmd, body=%wide.region_1.4_spmd.sunk | while | flops 205308048 | bytes 35166580 | solution.py:123
  213.3 10.4 %while.57 = (s32[]{:T(128)}, f32[48]{0:T(128)S(1)}, f32[3072,128]{1,0:T(8,128)}, f32[2,48]{1,0:T(2,128)S(1)}, f32[2,3072,128]{2,1,0:T(8,128)}, /*index=5*/f32[2,...) while((s32[]{:T(128)}, f32[48]{0:T(128)S(1)}, f32[3072,128]{1,0:T(8,128)}, ...), condition=%wide.region_6.7_spmd.clone, body=%wide.region_5.6_spmd.clone.sunk | while | flops 1572963 | bytes 20498576 | solution.py:137
  220.6 3.0 bitcast_add_fusion.4
  225.2 14.5 %all-reduce = f32[384]{0:T(512)S(1)} all-reduce(f32[384]{0:T(512)S(1)} %dynamic-update-slice), channel_id=2, replica_groups=mesh['dp'=4,'seq'=8] {'seq'}, use_global_device_ids=true, to_apply=%add | all-reduce | flops 384 | bytes 3072
  240.0 98.8 %all-gather.11.cloned.1.call-done = f32[24576,128]{1,0:T(8,128)} async-done(((f32[3072,128]{1,0:T(8,128)}), f32[24576,128]{1,0:T(8,128)}) %all-gather.11.cloned.1.call-update) | async-done | bytes 12582928 | tf_op jit(solution)/shard_map/all_gather | solution.py:12
  338.8 25.4 %while.58 = (s32[]{:T(128)}, f32[3072,128]{1,0:T(8,128)}, s32[]{:T(128)}, f32[8,48]{1,0:T(8,128)S(1)}, f32[8,3072,128]{2,1,0:T(8,128)}, /*index=5*/s32[]{:T(128)}, s32[]{:T(128)}) while((s32[]{:T(128)}, f32[3072,128]{1,0:T(8,128)}, s32[]{:T(128)}, f32[8,48]{1,0:T(8,128)S(1)}, f32[8,3072,128]{2,1,0:T(8,128)}, /*index=5*/s32[]{:T(128)}, ...), condition=%wide.region_8.9_spmd.clone, body=%wide.region_7.8_spmd.clone.sunk | while | flops 1572868 | bytes 4768425 | solution.py:21
  338.9 3.1 fusion.128
  342.1 3.5 fusion.128
  345.8 3.5 fusion.128
  349.5 3.5 fusion.128
  353.2 3.5 fusion.128
  356.9 3.5 fusion.128
  360.6 3.5 fusion.128
  364.1 3.7 multiply_add_fusion
  367.8 68.5 %while.56 = (s32[]{:T(128)}, bf16[2,256,3072]{2,1,0:T(8,128)(2,1)}, bf16[2,256,128]{2,1,0:T(8,128)(2,1)S(1)}, bf16[2,256,3072]{1,2,0:T(8,128)(2,1)}, bf16[2,256,...) while((s32[]{:T(128)}, bf16[2,256,3072]{2,1,0:T(8,128)(2,1)}, ...), condition=%wide.region_15.16_spmd, body=%wide.region_9.15_spmd.sunk | while | flops 1291211008 | bytes 81402336 | solution.py:146
  371.2 5.8 %multiply_reduce_fusion.4 = (f32[256,48]{0,1:T(8,128)S(1)}, f32[256,48,64]{0,2,1:T(8,128)}) fusion(f32[256,48,64]{0,2,1:T(8,128)S(1)} %fusion.122, f32[256,48]{0,1:T(8,128)S(1)} %exponential_bitcast_fusion.2, bf16[256,48,64]{0,2,1:T(8,128)(2,1)S(1)} %bitcast.241, f32[48,256]{1,0:T(8,128)S(1)} %dynamic-slice_bitcast_fusion.4, ...), kind=kOutput, calls=%fused_computation.46.clone.1 | convolution fusion | flops 421515264 | bytes 8388608 | tf_op jit(solution)/shard_map/while/body/eval_jaxpr/hts,shp->thp/dot_general | solution.py:63
  377.8 3.7 multiply_convert_fusion.8
  384.1 3.7 constant_dynamic-slice_fusion.9
  390.4 6.2 %multiply_convert_fusion.9 = (bf16[256,48,64]{0,2,1:T(8,128)(2,1)S(1)}, bf16[256,48,64]{0,2,1:T(8,128)(2,1)S(1)}) fusion(f32[256,48]{0,1:T(8,128)S(1)} %exponential_bitcast_fusion.2, f32[]{:T(128)} %bitcast.227, f32[256,48]{0,1:T(8,128)S(1)} %get-tuple-element.669, f32[256,48,64]{0,2,1:T(8,128)} %get-tuple-element.665, ...), kind=kOutput, calls=%fused_computation.44.clone.1 | output fusion | flops 10235967 | bytes 8024068 | tf_op jit(solution)/shard_map/while/body/eval_jaxpr/mul | solution.py:79
  396.7 4.6 multiply_reduce_fusion.5
  405.5 5.8 %multiply_reduce_fusion.4 = (f32[256,48]{0,1:T(8,128)S(1)}, f32[256,48,64]{0,2,1:T(8,128)}) fusion(f32[256,48,64]{0,2,1:T(8,128)S(1)} %fusion.122, f32[256,48]{0,1:T(8,128)S(1)} %exponential_bitcast_fusion.2, bf16[256,48,64]{0,2,1:T(8,128)(2,1)S(1)} %bitcast.241, f32[48,256]{1,0:T(8,128)S(1)} %dynamic-slice_bitcast_fusion.4, ...), kind=kOutput, calls=%fused_computation.46.clone.1 | convolution fusion | flops 421515264 | bytes 8388608 | tf_op jit(solution)/shard_map/while/body/eval_jaxpr/hts,shp->thp/dot_general | solution.py:63
  412.0 3.7 multiply_convert_fusion.8
  418.4 3.7 constant_dynamic-slice_fusion.9
  424.7 6.2 %multiply_convert_fusion.9 = (bf16[256,48,64]{0,2,1:T(8,128)(2,1)S(1)}, bf16[256,48,64]{0,2,1:T(8,128)(2,1)S(1)}) fusion(f32[256,48]{0,1:T(8,128)S(1)} %exponential_bitcast_fusion.2, f32[]{:T(128)} %bitcast.227, f32[256,48]{0,1:T(8,128)S(1)} %get-tuple-element.669, f32[256,48,64]{0,2,1:T(8,128)} %get-tuple-element.665, ...), kind=kOutput, calls=%fused_computation.44.clone.1 | output fusion | flops 10235967 | bytes 8024068 | tf_op jit(solution)/shard_map/while/body/eval_jaxpr/mul | solution.py:79
  430.9 4.6 multiply_reduce_fusion.5
  438.0 30.0 %reduce-scatter.4.cloned.1.call-done = bf16[320,128]{1,0:T(8,128)(2,1)} async-done(((bf16[2560,128]{1,0:T(8,128)(2,1)}), bf16[320,128]{1,0:T(8,128)(2,1)}) %reduce-scatter.4.cloned.1.call-update) | async-done | bytes 81936
  469.7 42.0 %all-reduce.3.cloned.1.call-done = bf16[320,128]{0,1:T(8,128)(2,1)} async-done(((bf16[320,128]{0,1:T(8,128)(2,1)}), bf16[320,128]{0,1:T(8,128)(2,1)}) %all-reduce.3.cloned.1.call-update) | async-done | bytes 81936 | tf_op jit(solution)/shard_map/psum | solution.py:169
  (176 shorter events, 56.5 us)
Async XLA Ops:
  7.2 19.4 %copy-start = (bf16[1,512,2560]{2,1,0:T(8,128)(2,1)S(1)}, bf16[1,512,2560]{2,1,0:T(8,128)(2,1)}, u32[]{:S(2)}) copy-start(bf16[1,512,2560]{2,1,0:T(8,128)(2,1)} %param.17) | copy-start | bytes 7864324
  7.2 18.1 %copy-start.10 = (f32[48]{0:T(128)S(1)}, f32[48]{0:T(128)}, u32[]{:S(2)}) copy-start(f32[48]{0:T(128)} %param.22) | copy-start | bytes 580
  7.2 18.1 %copy-start.11 = (s32[8]{0:T(128)S(1)}, s32[8]{0:T(128)}, u32[]{:S(2)}) copy-start(s32[8]{0:T(128)} %param.25) | copy-start | bytes 100
  7.2 19.4 %copy-start.9 = (f32[48]{0:T(128)S(1)}, f32[48]{0:T(128)}, u32[]{:S(2)}) copy-start(f32[48]{0:T(128)} %param.21) | copy-start | bytes 580
  7.2 29.2 %all-gather.9.cloned.1.call-start = ((), (), s32[]{:S(2)}) async-start(), calls=%async_computation.2 | async-start | bytes 1474560 | tf_op jit(solution)/shard_map/all_gather | solution.py:104
  7.9 172.1 %all-gather.7.cloned.1.call-start = ((), (), s32[]{:S(2)}) async-start(), calls=%async_computation.1 | async-start | bytes 17694720 | tf_op jit(solution)/shard_map/all_gather | solution.py:103
  8.7 330.1 %all-gather.11.cloned.1.call-start = ((), (), s32[]{:S(2)}) async-start(), calls=%async_computation.4 | async-start | bytes 14155776 | tf_op jit(solution)/shard_map/all_gather | solution.py:12
  200.7 2.4 copy-start.5
  203.6 1.7 copy-start.6
  206.7 2.4 copy-start.5
  209.6 1.7 copy-start.6
  213.3 10.5 %copy-start.12 = (u32[32]{0:T(128)S(1)}, u32[32]{0:T(128)}, u32[]{:S(2)}) copy-start(u32[32]{0:T(128)} %constant.99) | copy-start | bytes 388
  213.4 2.5 copy-start.7
  217.7 2.9 copy-start.7
  223.7 244.4 %reduce-scatter.4.cloned.1.call-start = ((), (), s32[]{:S(2)}) async-start(), calls=%async_computation.5 | async-start | bytes 737280
  364.1 3.7 copy-start.8
  368.7 2.3 copy-start.1
  371.1 5.9 %copy-start.3 = (bf16[1,256,3072]{1,2,0:T(8,128)(2,1)}, bf16[1,256,3072]{1,2,0:T(8,128)(2,1)S(1)}, u32[]{:S(2)}) copy-start(bf16[1,256,3072]{1,2,0:T(8,128)(2,1)S(1)} %constant_dynamic-slice_fusion.8) | copy-start | bytes 4718596 | tf_op jit(solution)/shard_map/while
  390.4 6.2 %copy-start.4 = (bf16[1,256,3072]{1,2,0:T(8,128)(2,1)S(1)}, bf16[1,256,3072]{1,2,0:T(8,128)(2,1)}, u32[]{:S(2)}) copy-start(bf16[1,256,3072]{1,2,0:T(8,128)(2,1)} %copy-done.3) | copy-start | bytes 4718596 | tf_op jit(solution)/shard_map/while
  396.6 4.8 copy-start.2
  402.9 2.3 copy-start.1
  405.4 5.9 %copy-start.3 = (bf16[1,256,3072]{1,2,0:T(8,128)(2,1)}, bf16[1,256,3072]{1,2,0:T(8,128)(2,1)S(1)}, u32[]{:S(2)}) copy-start(bf16[1,256,3072]{1,2,0:T(8,128)(2,1)S(1)} %constant_dynamic-slice_fusion.8) | copy-start | bytes 4718596 | tf_op jit(solution)/shard_map/while
  424.7 6.2 %copy-start.4 = (bf16[1,256,3072]{1,2,0:T(8,128)(2,1)S(1)}, bf16[1,256,3072]{1,2,0:T(8,128)(2,1)}, u32[]{:S(2)}) copy-start(bf16[1,256,3072]{1,2,0:T(8,128)(2,1)} %copy-done.3) | copy-start | bytes 4718596 | tf_op jit(solution)/shard_map/while
  430.9 4.8 copy-start.2
  438.0 73.7 %all-reduce.3.cloned.1.call-start = ((), (), s32[]{:S(2)}) async-start(), calls=%async_computation.3 | async-start | bytes 196608 | tf_op jit(solution)/shard_map/psum | solution.py:169
Sparse Core Ops, SparseCore 0:
  9.7 26.6 all-gather.8
  38.0 141.9 all-gather.6
  223.8 114.9 all-gather.10
  438.1 29.8 reduce-scatter.3
  471.4 40.3 all-reduce.2
where the time goes:
time: 521 us; the launch traced here: 520 us
  waiting for transfers between devices  322 us (62%)
  other arithmetic  62.6 us (12%)
  local copies, waits for them, and re-layouts  47.4 us (9%)
  matrix products  41.5 us (8%)
  blocking collectives  30.8 us (6%)
  between operations  14.6 us (3%)
    all_gather x1, waiting for transfers between devices, body(): lax.all_gather(w_x, 'seq', axis=0, tiled=True)  141 us
    all_gather x1, waiting for transfers between devices, entering(): pieces = jax.tree.map(lambda part: lax.all_gather(part, axis), value)  98.8 us
    psum x1, waiting for transfers between devices, body(): gradient = lax.psum(partial_rows, 'dp').astype(jnp.float32)  42 us
    unnamed x6, waiting for transfers between devices  31.4 us
    select_n x7, other arithmetic, hop(): jnp.where(position < mine, new, old)  24.3 us
    all_gather x1, blocking collectives, body(): lax.all_gather(w_dt, 'seq', axis=0, tiled=True)  16.2 us
    dynamic_slice x8, local copies, waits for them, and re-layouts, body(): lax.map(lambda stretch_data: stretch_state(stretch_data[0], stretch_data[...  16.2 us
    dot_general x3, matrix products, body(): jnp.dot(columns, block_rows, preferred_element_type=jnp.float32)  15.9 us
  transfers between devices with their start and end apart: 5, of which 5 were waited for; matrix products, arithmetic and copies ran while one was open for 1% of the time, Pallas kernels for 0%

commit v1 on v0

--- a/solution.py
+++ b/solution.py
@@ -166,7 +166,7 @@
         scatter_dimension=0,
         tiled=True,
     )
-    gradient = lax.psum(partial_rows, "dp").astype(jnp.float32)
+    gradient = jnp.sum(lax.all_gather(partial_rows, "dp"), axis=0).astype(jnp.float32)
     return (ssm_output[None], gradient)
 
 

time: 521 us -> 485 us (0.931)
  waiting for transfers between devices: 322 us -> 280 us
  blocking collectives: 30.8 us -> 40.3 us
    psum x1 -> x0, waiting for transfers between devices: 42 us -> none  [body(): gradient = lax.psum(partial_rows, 'dp').astype(jnp.float32)]
    reduce_scatter x0 -> x1, waiting for transfers between devices: none -> 30 us  [body(): lax.psum_scatter(jnp.dot(columns.T, grad_c_rows, preferred_element_type=j...]
    unnamed x6 -> x4, waiting for transfers between devices: 31.4 us -> 1.41 us
    all_gather x0 -> x1, blocking collectives: none -> 9.49 us  [body(): lax.all_gather(partial_rows, 'dp')]
  transfers between devices with their start and end apart: 5 -> 4, of which waited for: 5 -> 4; matrix products, arithmetic and copies ran while one was open for 1% -> 1% of each run, Pallas kernels for 0% -> 0%
where the time goes in v1:
time: 485 us
  waiting for transfers between devices  280 us (58%)
  other arithmetic  63.3 us (13%)
  local copies, waits for them, and re-layouts  44.1 us (9%)
  matrix products  41.5 us (9%)
  blocking collectives  40.3 us (8%)
  between operations  14.6 us (3%)
    all_gather x1, waiting for transfers between devices, body(): lax.all_gather(w_x, 'seq', axis=0, tiled=True)  141 us
    all_gather x1, waiting for transfers between devices, entering(): pieces = jax.tree.map(lambda part: lax.all_gather(part, axis), value)  98.8 us
    reduce_scatter x1, waiting for transfers between devices, body(): lax.psum_scatter(jnp.dot(columns.T, grad_c_rows, preferred_element_type=j...  30 us
    select_n x7, other arithmetic, hop(): jnp.where(position < mine, new, old)  24.3 us
    all_gather x1, blocking collectives, body(): lax.all_gather(w_dt, 'seq', axis=0, tiled=True)  16.2 us
    dynamic_slice x8, local copies, waits for them, and re-layouts, body(): lax.map(lambda stretch_data: stretch_state(stretch_data[0], stretch_data[...  16.2 us
    dot_general x3, matrix products, body(): jnp.dot(columns, block_rows, preferred_element_type=jnp.float32)  15.9 us
    unnamed x1, blocking collectives  14.5 us
  transfers between devices with their start and end apart: 4, of which 4 were waited for; matrix products, arithmetic and copies ran while one was open for 1% of the time, Pallas kernels for 0%

profile of v1, /device:TPU:0, one launch (start us, length us, event | category | flops | bytes accessed | tf_op | source)
XLA Modules:
  0.0 484.8 jit_solution(14596256720471039703)
XLA Ops:
  8.8 16.2 %all-gather.3 = bf16[8,320,48]{1,2,0:T(8,128)(2,1)S(1)} all-gather(bf16[1,320,48]{1,2,0:T(8,128)(2,1)} %bitcast.252), channel_id=1, replica_groups=mesh['dp'=4,'seq'=8] {'seq'}, dimensions={0}, use_global_device_ids=true | all-gather | bytes 276480 | tf_op jit(solution)/shard_map/all_gather | solution.py:105
  27.6 8.7 %all-gather.10.cloned.1.call-done = bf16[2560,256]{1,0:T(8,128)(2,1)} async-done(((bf16[320,256]{1,0:T(8,128)(2,1)}), bf16[2560,256]{1,0:T(8,128)(2,1)}) %all-gather.10.cloned.1.call-update) | async-done | bytes 1310736 | tf_op jit(solution)/shard_map/all_gather | solution.py:104
  38.6 141.5 %all-gather.8.cloned.1.call-done = bf16[2560,3072]{1,0:T(8,128)(2,1)} async-done(((bf16[320,3072]{1,0:T(8,128)(2,1)}), bf16[2560,3072]{1,0:T(8,128)(2,1)}) %all-gather.8.cloned.1.call-update) | async-done | bytes 15728656 | tf_op jit(solution)/shard_map/all_gather | solution.py:103
  180.1 12.8 %convolution_convert_fusion = bf16[512,3072]{1,0:T(8,128)(2,1)} fusion(bf16[2560,3072]{1,0:T(8,128)(2,1)} %all-gather.8.cloned.1.call-done, bf16[1,512,2560]{2,1,0:T(8,128)(2,1)S(1)} %copy-done), kind=kOutput, calls=%fused_computation.87 | convolution fusion | flops 8054636544 | bytes 21495808 | tf_op jit(solution)/shard_map/dot_general | solution.py:109
  192.9 4.7 copy.51
  199.4 11.9 %while.55 = (s32[]{:T(128)}, f32[2,48]{1,0:T(2,128)S(1)}, f32[2,3072,128]{2,1,0:T(8,128)}, f32[2,256,48]{1,2,0:T(8,128)S(1)}, f32[48]{0:T(128)S(1)}, /*index=5*/...) while((s32[]{:T(128)}, f32[2,48]{1,0:T(2,128)S(1)}, ...), condition=%wide.region_4.5_spmd, body=%wide.region_1.4_spmd.sunk | while | flops 205308048 | bytes 35166580 | solution.py:123
  213.3 10.4 %while.57 = (s32[]{:T(128)}, f32[48]{0:T(128)S(1)}, f32[3072,128]{1,0:T(8,128)}, f32[2,48]{1,0:T(2,128)S(1)}, f32[2,3072,128]{2,1,0:T(8,128)}, /*index=5*/f32[2,...) while((s32[]{:T(128)}, f32[48]{0:T(128)S(1)}, f32[3072,128]{1,0:T(8,128)}, ...), condition=%wide.region_6.7_spmd.clone, body=%wide.region_5.6_spmd.clone.sunk | while | flops 1572963 | bytes 20498576 | solution.py:137
  220.6 3.0 bitcast_add_fusion.4
  225.2 14.5 %all-reduce = f32[384]{0:T(512)S(1)} all-reduce(f32[384]{0:T(512)S(1)} %dynamic-update-slice), channel_id=2, replica_groups=mesh['dp'=4,'seq'=8] {'seq'}, use_global_device_ids=true, to_apply=%add | all-reduce | flops 384 | bytes 3072
  240.0 98.8 %all-gather.12.cloned.1.call-done = f32[24576,128]{1,0:T(8,128)} async-done(((f32[3072,128]{1,0:T(8,128)}), f32[24576,128]{1,0:T(8,128)}) %all-gather.12.cloned.1.call-update) | async-done | bytes 12582928 | tf_op jit(solution)/shard_map/all_gather | solution.py:12
  338.8 25.4 %while.58 = (s32[]{:T(128)}, f32[3072,128]{1,0:T(8,128)}, s32[]{:T(128)}, f32[8,48]{1,0:T(8,128)S(1)}, f32[8,3072,128]{2,1,0:T(8,128)}, /*index=5*/s32[]{:T(128)}, s32[]{:T(128)}) while((s32[]{:T(128)}, f32[3072,128]{1,0:T(8,128)}, s32[]{:T(128)}, f32[8,48]{1,0:T(8,128)S(1)}, f32[8,3072,128]{2,1,0:T(8,128)}, /*index=5*/s32[]{:T(128)}, ...), condition=%wide.region_8.9_spmd.clone, body=%wide.region_7.8_spmd.clone.sunk | while | flops 1572868 | bytes 4768425 | solution.py:21
  338.9 3.1 fusion.128
  342.1 3.5 fusion.128
  345.8 3.5 fusion.128
  349.5 3.5 fusion.128
  353.2 3.5 fusion.128
  356.9 3.5 fusion.128
  360.6 3.5 fusion.128
  364.1 3.7 multiply_add_fusion
  367.8 68.5 %while.56 = (s32[]{:T(128)}, bf16[2,256,3072]{2,1,0:T(8,128)(2,1)}, bf16[2,256,128]{2,1,0:T(8,128)(2,1)S(1)}, bf16[2,256,3072]{1,2,0:T(8,128)(2,1)}, bf16[2,256,...) while((s32[]{:T(128)}, bf16[2,256,3072]{2,1,0:T(8,128)(2,1)}, ...), condition=%wide.region_15.16_spmd, body=%wide.region_9.15_spmd.sunk | while | flops 1291211008 | bytes 81402336 | solution.py:146
  371.2 5.8 %multiply_reduce_fusion.4 = (f32[256,48]{0,1:T(8,128)S(1)}, f32[256,48,64]{0,2,1:T(8,128)}) fusion(f32[256,48,64]{0,2,1:T(8,128)S(1)} %fusion.122, f32[256,48]{0,1:T(8,128)S(1)} %exponential_bitcast_fusion.2, bf16[256,48,64]{0,2,1:T(8,128)(2,1)S(1)} %bitcast.242, f32[48,256]{1,0:T(8,128)S(1)} %dynamic-slice_bitcast_fusion.4, ...), kind=kOutput, calls=%fused_computation.46.clone.1 | convolution fusion | flops 421515264 | bytes 8388608 | tf_op jit(solution)/shard_map/while/body/eval_jaxpr/hts,shp->thp/dot_general | solution.py:63
  377.8 3.7 multiply_convert_fusion.8
  384.1 3.7 constant_dynamic-slice_fusion.9
  390.4 6.2 %multiply_convert_fusion.9 = (bf16[256,48,64]{0,2,1:T(8,128)(2,1)S(1)}, bf16[256,48,64]{0,2,1:T(8,128)(2,1)S(1)}) fusion(f32[256,48]{0,1:T(8,128)S(1)} %exponential_bitcast_fusion.2, f32[]{:T(128)} %bitcast.228, f32[256,48]{0,1:T(8,128)S(1)} %get-tuple-element.661, f32[256,48,64]{0,2,1:T(8,128)} %get-tuple-element.657, ...), kind=kOutput, calls=%fused_computation.44.clone.1 | output fusion | flops 10235967 | bytes 8024068 | tf_op jit(solution)/shard_map/while/body/eval_jaxpr/mul | solution.py:79
  396.7 4.6 multiply_reduce_fusion.5
  405.5 5.8 %multiply_reduce_fusion.4 = (f32[256,48]{0,1:T(8,128)S(1)}, f32[256,48,64]{0,2,1:T(8,128)}) fusion(f32[256,48,64]{0,2,1:T(8,128)S(1)} %fusion.122, f32[256,48]{0,1:T(8,128)S(1)} %exponential_bitcast_fusion.2, bf16[256,48,64]{0,2,1:T(8,128)(2,1)S(1)} %bitcast.242, f32[48,256]{1,0:T(8,128)S(1)} %dynamic-slice_bitcast_fusion.4, ...), kind=kOutput, calls=%fused_computation.46.clone.1 | convolution fusion | flops 421515264 | bytes 8388608 | tf_op jit(solution)/shard_map/while/body/eval_jaxpr/hts,shp->thp/dot_general | solution.py:63
  412.0 3.7 multiply_convert_fusion.8
  418.4 3.7 constant_dynamic-slice_fusion.9
  424.7 6.2 %multiply_convert_fusion.9 = (bf16[256,48,64]{0,2,1:T(8,128)(2,1)S(1)}, bf16[256,48,64]{0,2,1:T(8,128)(2,1)S(1)}) fusion(f32[256,48]{0,1:T(8,128)S(1)} %exponential_bitcast_fusion.2, f32[]{:T(128)} %bitcast.228, f32[256,48]{0,1:T(8,128)S(1)} %get-tuple-element.661, f32[256,48,64]{0,2,1:T(8,128)} %get-tuple-element.657, ...), kind=kOutput, calls=%fused_computation.44.clone.1 | output fusion | flops 10235967 | bytes 8024068 | tf_op jit(solution)/shard_map/while/body/eval_jaxpr/mul | solution.py:79
  430.9 4.6 multiply_reduce_fusion.5
  438.0 30.0 %reduce-scatter.4.cloned.1.call-done = bf16[320,128]{1,0:T(8,128)(2,1)} async-done(((bf16[2560,128]{1,0:T(8,128)(2,1)}), bf16[320,128]{1,0:T(8,128)(2,1)}) %reduce-scatter.4.cloned.1.call-update) | async-done | bytes 81936 | tf_op jit(solution)/shard_map/reduce_scatter | solution.py:163
  468.0 9.5 %all-gather.2 = bf16[1280,128]{1,0:T(8,128)(2,1)S(1)} all-gather(bf16[320,128]{1,0:T(8,128)(2,1)} %reduce-scatter.4.cloned.1.call-done), channel_id=4, replica_groups=mesh['dp'=4,'seq'=8] {'dp'}, dimensions={0}, use_global_device_ids=true | all-gather | bytes 409600 | tf_op jit(solution)/shard_map/all_gather | solution.py:169
  (174 shorter events, 53.9 us)
Async XLA Ops:
  7.2 19.4 %copy-start = (bf16[1,512,2560]{2,1,0:T(8,128)(2,1)S(1)}, bf16[1,512,2560]{2,1,0:T(8,128)(2,1)}, u32[]{:S(2)}) copy-start(bf16[1,512,2560]{2,1,0:T(8,128)(2,1)} %param.17) | copy-start | bytes 7864324
  7.2 18.1 %copy-start.10 = (f32[48]{0:T(128)S(1)}, f32[48]{0:T(128)}, u32[]{:S(2)}) copy-start(f32[48]{0:T(128)} %param.22) | copy-start | bytes 580
  7.2 18.1 %copy-start.11 = (s32[8]{0:T(128)S(1)}, s32[8]{0:T(128)}, u32[]{:S(2)}) copy-start(s32[8]{0:T(128)} %param.25) | copy-start | bytes 100
  7.2 19.4 %copy-start.9 = (f32[48]{0:T(128)S(1)}, f32[48]{0:T(128)}, u32[]{:S(2)}) copy-start(f32[48]{0:T(128)} %param.21) | copy-start | bytes 580
  7.2 29.2 %all-gather.10.cloned.1.call-start = ((), (), s32[]{:S(2)}) async-start(), calls=%async_computation.2 | async-start | bytes 1474560 | tf_op jit(solution)/shard_map/all_gather | solution.py:104
  7.9 172.1 %all-gather.8.cloned.1.call-start = ((), (), s32[]{:S(2)}) async-start(), calls=%async_computation.1 | async-start | bytes 17694720 | tf_op jit(solution)/shard_map/all_gather | solution.py:103
  8.7 330.1 %all-gather.12.cloned.1.call-start = ((), (), s32[]{:S(2)}) async-start(), calls=%async_computation.3 | async-start | bytes 14155776 | tf_op jit(solution)/shard_map/all_gather | solution.py:12
  200.7 2.4 copy-start.5
  203.6 1.7 copy-start.6
  206.7 2.4 copy-start.5
  209.6 1.7 copy-start.6
  213.3 10.5 %copy-start.12 = (u32[32]{0:T(128)S(1)}, u32[32]{0:T(128)}, u32[]{:S(2)}) copy-start(u32[32]{0:T(128)} %constant.101) | copy-start | bytes 388
  213.4 2.5 copy-start.7
  217.7 2.9 copy-start.7
  223.7 244.4 %reduce-scatter.4.cloned.1.call-start = ((), (), s32[]{:S(2)}) async-start(), calls=%async_computation.4 | async-start | bytes 737280 | tf_op jit(solution)/shard_map/reduce_scatter | solution.py:163
  364.1 3.7 copy-start.8
  368.7 2.3 copy-start.1
  371.1 5.9 %copy-start.3 = (bf16[1,256,3072]{1,2,0:T(8,128)(2,1)}, bf16[1,256,3072]{1,2,0:T(8,128)(2,1)S(1)}, u32[]{:S(2)}) copy-start(bf16[1,256,3072]{1,2,0:T(8,128)(2,1)S(1)} %constant_dynamic-slice_fusion.8) | copy-start | bytes 4718596 | tf_op jit(solution)/shard_map/while
  390.4 6.2 %copy-start.4 = (bf16[1,256,3072]{1,2,0:T(8,128)(2,1)S(1)}, bf16[1,256,3072]{1,2,0:T(8,128)(2,1)}, u32[]{:S(2)}) copy-start(bf16[1,256,3072]{1,2,0:T(8,128)(2,1)} %copy-done.3) | copy-start | bytes 4718596 | tf_op jit(solution)/shard_map/while
  396.6 4.8 copy-start.2
  402.9 2.3 copy-start.1
  405.4 5.9 %copy-start.3 = (bf16[1,256,3072]{1,2,0:T(8,128)(2,1)}, bf16[1,256,3072]{1,2,0:T(8,128)(2,1)S(1)}, u32[]{:S(2)}) copy-start(bf16[1,256,3072]{1,2,0:T(8,128)(2,1)S(1)} %constant_dynamic-slice_fusion.8) | copy-start | bytes 4718596 | tf_op jit(solution)/shard_map/while
  424.7 6.2 %copy-start.4 = (bf16[1,256,3072]{1,2,0:T(8,128)(2,1)S(1)}, bf16[1,256,3072]{1,2,0:T(8,128)(2,1)}, u32[]{:S(2)}) copy-start(bf16[1,256,3072]{1,2,0:T(8,128)(2,1)} %copy-done.3) | copy-start | bytes 4718596 | tf_op jit(solution)/shard_map/while
  430.9 4.8 copy-start.2
Sparse Core Ops, SparseCore 0:
  9.7 26.6 all-gather.9
  38.0 141.9 all-gather.7
  223.8 114.9 all-gather.11
  438.1 29.8 reduce-scatter.3
